TPU v7x, 512 devices: a 4x2x32 block of a 4x8x32 slice. The times are simulated.
512 devices in a mesh: groups: 2 (over y), ep: 32 (over z), tp: 4 (over x), dp: 2 (over core).
Axes of the slice: x: 4, y: 2, z: 32, core: 2. Of those that a mesh axis runs over, the one named last changes fastest.
The devices are a block of a 4x8x32 slice.
Arguments:
- tokens: bfloat16 [4096, 5120], P(('groups', 'ep', 'tp', 'dp')), parts along dimension 0, may hold values from -6 to 6
- route_weights: float32 [4096, 8], P(('groups', 'ep', 'tp', 'dp')), parts along dimension 0, may hold values from 0.1 to 1
- expert_ids: int32 [4096, 8], P(('groups', 'ep', 'tp', 'dp')), parts along dimension 0, may hold values from 0 to 31, all different within a row; in each aligned block of 8 rows (0 to 7, 8 to 15, ...) at most 4 rows name the same one
- gate_weight: bfloat16 [32, 5120, 1024], P('ep', None, ('tp', 'dp')), may hold values from -0.078125 to 0.078125
- up_weight: bfloat16 [32, 5120, 1024], P('ep', None, ('tp', 'dp')), may hold values from -0.078125 to 0.078125
- down_weight: bfloat16 [32, 1024, 5120], P('ep', None, ('tp', 'dp')), may hold values from -0.1875 to 0.1875
Outputs:
- combined: bfloat16 [4096, 5120], P(('groups', 'ep', 'tp', 'dp')), parts along dimension 0
There are 2 independent parts, one for each index of `groups`. A program takes and returns all parts, laid end to end along the dimension named above; an argument that names none is the same for every part. Nothing has to cross between parts.
Inputs may be any that keep to these rules, and one draw needn't show every extreme that they name: `expert_ids`: each row names 8 different experts. Among the 8 rows of one device no expert is named more than 4 times, and in every draw some device's rows name some expert exactly 4 times.
All inputs are finite; a program needn't handle non-finite values.
Results may differ from a plain program's by a relative error of at most 0.0057.
Values may be sent and summed in bfloat16 or wider, within the bound.
A program may use at most 64 MiB of HBM per device.

v0:
```python
import jax
import jax.numpy as jnp
from jax import lax
from jax.sharding import PartitionSpec as P

CAP = 4


def sent_to_all(x, axis):
    size = lax.axis_size(axis)
    return lax.all_to_all(jnp.broadcast_to(x[None], (size, *x.shape)), axis, 0, 0, tiled=True)


def laid_out(tiles, dim):
    tiles = jnp.moveaxis(tiles, 0, dim)
    lengths = tiles.shape
    return tiles.reshape(*lengths[:dim], lengths[dim] * lengths[dim + 1], *lengths[dim + 2 :])


def gathered_copies(x, axis, dim):
    tiles = sent_to_all(x, axis)
    return laid_out(tiles, dim)


def route_table(ids, experts, capacity):
    tok_count, top_count = ids.shape
    flat = ids.reshape(-1)
    onehot = (flat[:, None] == jnp.arange(experts, dtype=jnp.int32)[None, :]).astype(jnp.int32)
    slots = jnp.sum(onehot * jnp.cumsum(onehot, axis=0), axis=1) - 1
    place = flat * capacity + slots
    owner = jnp.arange(tok_count * top_count, dtype=jnp.int32) // top_count
    table = jnp.full((experts * capacity,), tok_count, jnp.int32).at[place].set(owner)
    return (place, table)


def per_device(tokens, route_weights, expert_ids, gate_weight, up_weight, down_weight):
    n_owner = lax.axis_size("ep")
    tok_count, top_count = expert_ids.shape
    exp_local = gate_weight.shape[0]
    experts = exp_local * n_owner
    width = tokens.shape[1]
    place, table = route_table(expert_ids, experts, CAP)
    sendbuf = jnp.take(tokens, table, axis=0, mode="fill", fill_value=0).reshape(
        experts, CAP, width
    )
    arrived = lax.all_to_all(sendbuf, "ep", split_axis=0, concat_axis=0, tiled=True)
    arrived = arrived.reshape(1, n_owner, exp_local, CAP, width)
    piece = lax.all_gather(arrived, ("tp", "dp"), axis=0, tiled=True)
    gate = jnp.einsum("gsecd,edf->gsecf", piece, gate_weight, preferred_element_type=jnp.float32)
    up = jnp.einsum("gsecd,edf->gsecf", piece, up_weight, preferred_element_type=jnp.float32)
    hidden = (jax.nn.silu(gate) * up).astype(jnp.bfloat16)
    partial_out = jnp.einsum(
        "gsecf,efd->gsecd",
        gathered_copies(hidden, ("tp", "dp"), 4),
        down_weight,
        preferred_element_type=jnp.float32,
    )
    expert_out = partial_out.astype(jnp.bfloat16)
    mine = lax.all_to_all(expert_out, ("tp", "dp"), split_axis=0, concat_axis=4, tiled=True)
    mine = mine.reshape(n_owner * exp_local, CAP, width)
    returned = lax.all_to_all(mine, "ep", split_axis=0, concat_axis=0, tiled=True)
    picked = jnp.take(returned.reshape(experts * CAP, width), place, axis=0)
    picked = picked.reshape(tok_count, top_count, width).astype(jnp.float32)
    combined = jnp.sum(picked * route_weights[:, :, None], axis=1)
    return combined.astype(jnp.bfloat16)


def solution(mesh):
    return jax.shard_map(
        per_device,
        mesh=mesh,
        in_specs=(
            P(("groups", "ep", "tp", "dp"), None),
            P(("groups", "ep", "tp", "dp"), None),
            P(("groups", "ep", "tp", "dp"), None),
            P("ep", None, ("tp", "dp")),
            P("ep", None, ("tp", "dp")),
            P("ep", None, ("tp", "dp")),
        ),
        out_specs=P(("groups", "ep", "tp", "dp"), None),
        check_vma=False,
    )
```

profile of v0, /device:TPU:40, one launch (start us, length us, event | category | flops | bytes accessed | tf_op | source)
XLA Modules:
  0.0 481.4 jit_solution(17213974278287138052)
XLA Ops:
  6.6 0.9 reshape.101
  7.4 0.7 broadcast_multiply_fusion
  8.1 0.1 fusion.33
  8.2 0.1 reduce_window_sum.11
  8.3 0.2 select_reduce_fusion
  8.5 0.1 mul.40
  8.6 0.8 scatter_custom_fusion
  9.4 1.3 gather_fusion
  10.7 1.4 gather.13
  12.1 0.1 broadcast_in_dim.40
  12.2 2.0 broadcast_select_fusion
  14.2 177.4 %all_to_all.30 = bf16[32,4,5120]{2,1,0:T(4,128)(2,1)S(1)} all-to-all(bf16[32,4,5120]{2,1,0:T(4,128)(2,1)S(1)} %broadcast_select_fusion), channel_id=1, replica_groups=mesh['groups'=2,'ep'=32,'tp'=4,'dp'=2] {'ep'}, dimensions={0} | all-to-all | bytes 2621440 | tf_op jit(solution)/shard_map/all_to_all | solution.py:46
  191.6 1.5 copy.13
  193.2 56.3 %all-gather.3.cloned.1.call-done = bf16[256,4,5120]{2,0,1:T(8,128)(2,1)} async-done(((bf16[32,4,5120]{2,0,1:T(8,128)(2,1)}), bf16[256,4,5120]{2,0,1:T(8,128)(2,1)}) %all-gather.3.cloned.1.call-update) | async-done | bytes 10485776 | tf_op jit(solution)/shard_map/all_gather | solution.py:48
  249.5 5.8 %fusion.8 = f32[8,32,1,4,128]{4,1,3,0,2:T(8,128)S(1)} fusion(bf16[1,5120,128]{2,1,0:T(8,128)(2,1)S(1)} %copy-done.5, bf16[8,32,4,5120]{3,1,0,2:T(8,128)(2,1)} %bitcast.85), kind=kOutput, calls=%fused_computation.14 | convolution fusion | flops 1342177280 | bytes 12320768 | tf_op jit(solution)/shard_map/gsecd,edf->gsecf/dot_general | solution.py:49
  255.3 1.3 copy-done.4
  256.5 0.3 copy-done.6
  256.9 2.9 fusion.28
  259.7 0.5 broadcast_in_dim.45
  260.2 30.3 %all_to_all.31 = bf16[8,8,32,1,4,128]{5,2,4,1,3,0:T(8,128)(2,1)S(1)} all-to-all(bf16[8,8,32,1,4,128]{5,2,4,1,3,0:T(8,128)(2,1)S(1)} %broadcast_in_dim.45), channel_id=1, replica_groups=mesh['groups'=2,'ep'=32,'tp'=4,'dp'=2] {'tp','dp'}, dimensions={0} | all-to-all | bytes 4194304 | tf_op jit(solution)/shard_map/all_to_all | solution.py:11
  290.5 2.5 copy.16
  293.0 2.3 reshape.106
  295.3 3.4 fusion.4
  298.7 21.5 %all_to_all.32 = bf16[8,32,1,4,640]{4,1,3,2,0:T(8,128)(2,1)S(1)} all-to-all(bf16[8,32,1,4,640]{4,1,3,2,0:T(8,128)(2,1)S(1)} %fusion.4), channel_id=1, replica_groups=mesh['groups'=2,'ep'=32,'tp'=4,'dp'=2] {'tp','dp'}, dimensions={0} | all-to-all | bytes 2621440 | tf_op jit(solution)/shard_map/all_to_all | solution.py:59
  320.2 0.7 copy.23
  320.9 1.3 reshape.140
  322.2 23.6 %all-to-all-start.3 = ((bf16[32,4,5120]{2,1,0:T(4,128)(2,1)}), bf16[32,4,5120]{2,1,0:T(4,128)(2,1)}, u32[]{:S(2)}, u32[]{:S(2)}) async-start(bf16[32,4,5120]{2,1,0:T(4,128)(2,1)} %reshape.140), calls=%async_computation.3 | async-start | bytes 2621440 | tf_op jit(solution)/shard_map/all_to_all | solution.py:61
  345.8 0.1 sub.15
  345.9 124.0 %all-to-all-done.3 = bf16[32,4,5120]{2,1,0:T(4,128)(2,1)} async-done(((bf16[32,4,5120]{2,1,0:T(4,128)(2,1)}), bf16[32,4,5120]{2,1,0:T(4,128)(2,1)}, u32[]{:S(2)}, u32[]{:S(2)}) %all-to-all-start.3) | async-done | bytes 1310752 | tf_op jit(solution)/shard_map/all_to_all | solution.py:61
  469.9 2.5 reshape.109
  472.4 0.9 gather_fusion.1
  473.3 1.2 multiply_reduce_fusion
  (22 shorter events, 0.1 us)
Async XLA Ops:
  6.5 288.8 %copy-start = (bf16[1,1024,640]{2,1,0:T(8,128)(2,1)S(1)}, bf16[1,1024,640]{2,1,0:T(8,128)(2,1)}, u32[]{:S(2)}) copy-start(bf16[1,1024,640]{2,1,0:T(8,128)(2,1)} %param.11) | copy-start | bytes 3932164
  6.6 2.9 copy-start.1
  6.6 243.0 %all-gather.3.cloned.1.call-start = ((), (), s32[]{:S(2)}) async-start(), calls=%async_computation.4 | async-start | bytes 11796480 | tf_op jit(solution)/shard_map/all_gather | solution.py:48
  193.1 56.4 %copy-start.5 = (bf16[1,5120,128]{2,1,0:T(8,128)(2,1)S(1)}, bf16[1,5120,128]{2,1,0:T(8,128)(2,1)}, u32[]{:S(2)}) copy-start(bf16[1,5120,128]{2,1,0:T(8,128)(2,1)} %param.9) | copy-start | bytes 3932164
  249.5 7.0 %copy-start.4 = (bf16[256,4,5120]{2,0,1:T(8,128)(2,1)S(1)}, bf16[256,4,5120]{2,0,1:T(8,128)(2,1)}, u32[]{:S(2)}) copy-start(bf16[256,4,5120]{2,0,1:T(8,128)(2,1)} %all-gather.3.cloned.1.call-done) | copy-start | bytes 31457284
  249.5 7.3 %copy-start.6 = (bf16[1,5120,128]{2,1,0:T(8,128)(2,1)S(1)}, bf16[1,5120,128]{2,1,0:T(8,128)(2,1)}, u32[]{:S(2)}) copy-start(bf16[1,5120,128]{2,1,0:T(8,128)(2,1)} %param.10) | copy-start | bytes 3932164
  322.2 23.7 %copy-start.2 = (s32[8,8]{1,0:T(8,128)S(1)}, s32[8,8]{1,0:T(8,128)}, u32[]{:S(2)}) copy-start(s32[8,8]{1,0:T(8,128)} %param.8) | copy-start | bytes 772
  322.2 147.7 %all-to-all-start.3 = ((bf16[32,4,5120]{2,1,0:T(4,128)(2,1)}), bf16[32,4,5120]{2,1,0:T(4,128)(2,1)}, u32[]{:S(2)}, u32[]{:S(2)}) async-start(bf16[32,4,5120]{2,1,0:T(4,128)(2,1)} %reshape.140), calls=%async_computation.3 | async-start | bytes 2621440 | tf_op jit(solution)/shard_map/all_to_all | solution.py:61
  472.4 0.9 copy-start.3
Sparse Core Ops, SparseCore 0:
  193.3 56.1 all-gather.2
where the time goes:
time: 483 us; the launch traced here: 481 us
  blocking collectives  229 us (47%)
  waiting for transfers between devices  180 us (37%)
  starting transfers between devices  23.6 us (5%)
  local copies, waits for them, and re-layouts  18.3 us (4%)
  between operations  13.6 us (3%)
  matrix products  12 us (2%)
    all_to_all x1, blocking collectives, per_device(): lax.all_to_all(sendbuf, 'ep', split_axis=0, concat_axis=0, tiled=True)  177 us
    all_to_all x1, waiting for transfers between devices, per_device(): lax.all_to_all(mine, 'ep', split_axis=0, concat_axis=0, tiled=True)  124 us
    all_gather x1, waiting for transfers between devices, per_device(): piece = lax.all_gather(arrived, ('tp', 'dp'), axis=0, tiled=True)  56.3 us
    all_to_all x1, blocking collectives, sent_to_all(): lax.all_to_all(jnp.broadcast_to(x[None], (size, *x.shape)), axis, 0, 0, t...  30.3 us
    all_to_all x1, starting transfers between devices, per_device(): lax.all_to_all(mine, 'ep', split_axis=0, concat_axis=0, tiled=True)  23.6 us
    all_to_all x1, blocking collectives, per_device(): lax.all_to_all(expert_out, ('tp', 'dp'), split_axis=0, concat_axis=4, til...  21.5 us
  transfers between devices with their start and end apart: 2, of which 2 were waited for; matrix products, arithmetic and copies ran while one was open for 0% of the time, Pallas kernels for 0%

commit v1 on v0

v1 whole, which is shorter than its diff:
```python
import jax
import jax.numpy as jnp
from jax import lax
from jax.sharding import PartitionSpec as P

CAP = 4
META = 128


def pieces(w):
    hi = w.astype(jnp.bfloat16)
    rest = w - hi.astype(jnp.float32)
    mid = rest.astype(jnp.bfloat16)
    low = (rest - mid.astype(jnp.float32)).astype(jnp.bfloat16)
    return jnp.concatenate([hi, mid, low], axis=-1)


def per_device(tokens, route_weights, expert_ids, gate_weight, up_weight, down_weight):
    n_ep = lax.axis_size("ep")
    rows, width = tokens.shape
    named = expert_ids[:, :, None] == jnp.arange(n_ep, dtype=jnp.int32)[None, None, :]
    dense = jnp.sum(jnp.where(named, route_weights[:, :, None], 0.0), axis=1)
    eye = jnp.eye(rows, dtype=jnp.bfloat16)
    meta = jnp.concatenate([pieces(dense), eye], axis=1)
    meta = jnp.pad(meta, ((0, 0), (0, META - meta.shape[1])))
    sent = jnp.concatenate([tokens, meta], axis=1)
    got = lax.all_gather(sent, "ep", axis=0)
    me = lax.axis_index("ep")

    def weight_of(block):
        m = block[..., width:].astype(jnp.float32)
        part = [lax.dynamic_slice_in_dim(m, me + j * n_ep, 1, axis=-1) for j in range(3)]
        return (part[0] + part[1] + part[2])[..., 0]

    mask = weight_of(got) > 0
    slot = jnp.cumsum(mask.astype(jnp.int32), axis=1) - 1
    pick = mask[:, None, :] & (slot[:, None, :] == jnp.arange(CAP)[None, :, None])
    sel = jnp.einsum("bst,btd->bsd", pick.astype(jnp.bfloat16), got, preferred_element_type=jnp.bfloat16)
    piece = lax.all_gather(sel, ("tp", "dp"), axis=0)
    x = piece[..., :width]
    gate = jnp.einsum("gbsd,df->gbsf", x, gate_weight[0], preferred_element_type=jnp.float32)
    up = jnp.einsum("gbsd,df->gbsf", x, up_weight[0], preferred_element_type=jnp.float32)
    hidden = (jax.nn.silu(gate) * up).astype(jnp.bfloat16)
    hidden = lax.all_gather(hidden, ("tp", "dp"), axis=3, tiled=True)
    out = jnp.einsum("gbsf,fd->gbsd", hidden, down_weight[0], preferred_element_type=jnp.float32).astype(jnp.bfloat16)
    code = piece[..., width + 3 * n_ep : width + 3 * n_ep + rows]
    w = weight_of(piece)
    w_tok = jnp.sum(code.astype(jnp.float32) * w[..., None], axis=2)
    back = jnp.einsum("gbst,gbsd->bgtd", code, out, preferred_element_type=jnp.float32)
    back = (back * jnp.swapaxes(w_tok, 0, 1)[..., None]).astype(jnp.bfloat16)
    flat = back.reshape(n_ep * back.shape[1] * rows, back.shape[3])
    summed = lax.psum_scatter(flat, "ep", scatter_dimension=0, tiled=True)
    summed = summed.reshape(back.shape[1], rows, back.shape[3])
    mine = lax.all_to_all(summed, ("tp", "dp"), split_axis=0, concat_axis=2, tiled=True)
    return mine[0]


def solution(mesh):
    tok = P(("groups", "ep", "tp", "dp"), None)
    wgt = P("ep", None, ("tp", "dp"))
    return jax.shard_map(
        per_device,
        mesh=mesh,
        in_specs=(tok, tok, tok, wgt, wgt, wgt),
        out_specs=tok,
        check_vma=False,
    )
```

time: 483 us -> 467 us (0.967)
  waiting for transfers between devices: 180 us -> 408 us
  blocking collectives: 229 us -> 10 us
  starting transfers between devices: 23.6 us -> 0.2 us
  local copies, waits for them, and re-layouts: 18.3 us -> 12.9 us
    all_to_all x3 -> x1, blocking collectives: 229 us -> 10 us  [per_device(): lax.all_to_all(summed, ('tp', 'dp'), split_axis=0, concat_axis=2, tiled=T...]
    all_gather x1 -> x3, waiting for transfers between devices: 56.3 us -> 268 us  [the longest x1 162 us: per_device(): got = lax.all_gather(sent, 'ep', axis=0)]
    reduce_scatter x0 -> x1, waiting for transfers between devices: none -> 139 us  [per_device(): summed = lax.psum_scatter(flat, 'ep', scatter_dimension=0, tiled=True)]
    all_to_all x1 -> x0, waiting for transfers between devices: 124 us -> none  [per_device(): lax.all_to_all(mine, 'ep', split_axis=0, concat_axis=0, tiled=True)]
    all_to_all x1 -> x0, starting transfers between devices: 23.6 us -> none  [per_device(): lax.all_to_all(mine, 'ep', split_axis=0, concat_axis=0, tiled=True)]
    all_gather x0 -> x1, local copies, waits for them, and re-layouts: none -> 7.13 us  [per_device(): piece = lax.all_gather(sel, ('tp', 'dp'), axis=0)]
    reshape x4 -> x0, local copies, waits for them, and re-layouts: 5.34 us -> none  [the longest x1 2.46 us: per_device(): picked = jnp.take(returned.reshape(experts * CAP, width), place, axis=0)]
    dot_general x3 -> x5, matrix products: 12 us -> 16.6 us  [the longest x1 3.72 us: per_device(): jnp.einsum('gbsd,df->gbsf', x, up_weight[0], preferred_element_type=jnp.f...]
  transfers between devices with their start and end apart: 2 -> 4, of which waited for: 2 -> 4; matrix products, arithmetic and copies ran while one was open for 0% -> 1% of each run, Pallas kernels for 0% -> 0%
where the time goes in v1:
time: 467 us; the launch traced here: 465 us
  waiting for transfers between devices  408 us (87%)
  matrix products  16.6 us (4%)
  between operations  13.3 us (3%)
  local copies, waits for them, and re-layouts  12.9 us (3%)
  blocking collectives  10 us (2%)
    all_gather x1, waiting for transfers between devices, per_device(): got = lax.all_gather(sent, 'ep', axis=0)  162 us
    reduce_scatter x1, waiting for transfers between devices, per_device(): summed = lax.psum_scatter(flat, 'ep', scatter_dimension=0, tiled=True)  139 us
    all_gather x1, waiting for transfers between devices, per_device(): piece = lax.all_gather(sel, ('tp', 'dp'), axis=0)  66.6 us
    all_gather x1, waiting for transfers between devices, per_device(): hidden = lax.all_gather(hidden, ('tp', 'dp'), axis=3, tiled=True)  38.9 us
    all_to_all x1, blocking collectives, per_device(): lax.all_to_all(summed, ('tp', 'dp'), split_axis=0, concat_axis=2, tiled=T...  10 us
  transfers between devices with their start and end apart: 4, of which 4 were waited for; matrix products, arithmetic and copies ran while one was open for 1% of the time, Pallas kernels for 0%

profile of v1, /device:TPU:40, one launch (start us, length us, event | category | flops | bytes accessed | tf_op | source)
XLA Modules:
  0.0 465.1 jit_solution(3061447939570187865)
XLA Ops:
  6.6 0.9 select_reduce_fusion
  7.5 0.1 fusion.33
  7.6 1.5 pad_maximum_fusion
  9.1 0.1 all-gather.8.cloned.1.call-update
  9.1 0.1 all-gather.10.cloned.1.call-start
  9.2 162.4 %all-gather.8.cloned.1.call-done = bf16[256,5248]{1,0:T(8,128)(2,1)} async-done(((bf16[8,5248]{1,0:T(8,128)(2,1)}), bf16[256,5248]{1,0:T(8,128)(2,1)}) %all-gather.8.cloned.1.call-update) | async-done | bytes 2686992 | tf_op jit(solution)/shard_map/all_gather | solution.py:27
  171.6 0.8 slice.16
  172.5 0.2 copy.60
  172.8 0.1 copy.49
  172.9 0.1 copy.50
  173.0 3.7 fusion.20
  176.7 0.1 all-gather.10.cloned.1.call-update
  176.7 0.1 all-gather.6.cloned.1.call-start
  176.8 66.6 %all-gather.10.cloned.1.call-done = bf16[256,4,5248]{2,1,0:T(4,128)(2,1)} async-done(((bf16[32,4,5248]{2,1,0:T(4,128)(2,1)}), bf16[256,4,5248]{2,1,0:T(4,128)(2,1)}) %all-gather.10.cloned.1.call-update) | async-done | bytes 10747920 | tf_op jit(solution)/shard_map/all_gather | solution.py:39
  243.5 7.1 %copy.51 = bf16[256,4,5248]{2,0,1:T(8,128)(2,1)S(1)} copy(bf16[256,4,5248]{2,1,0:T(4,128)(2,1)} %all-gather.10.cloned.1.call-done) | data formatting | bytes 21495808 | tf_op jit(solution)/shard_map/all_gather | solution.py:39
  250.6 2.9 fusion.2
  253.5 1.2 copy-done.1
  254.7 3.7 fusion.13
  258.4 0.1 all-gather.6.cloned.1.call-update
  258.4 0.1 reduce-scatter.2.cloned.1.call-start
  258.5 1.1 slice.17
  259.6 1.0 slice_convert_fusion
  260.6 0.5 dynamic-slice_add_fusion
  261.1 1.6 copy.59
  262.7 0.5 multiply_reduce_fusion
  263.3 38.9 %all-gather.6.cloned.1.call-done = bf16[8,32,4,1024]{3,1,2,0:T(8,128)(2,1)} async-done(((bf16[8,32,4,128]{3,1,2,0:T(8,128)(2,1)}), bf16[8,32,4,1024]{3,1,2,0:T(8,128)(2,1)}) %all-gather.6.cloned.1.call-update) | async-done | bytes 2097168 | tf_op jit(solution)/shard_map/all_gather | solution.py:44
  302.1 3.4 convolution_convert_fusion
  305.5 3.0 multiply_convert_fusion
  308.5 0.1 reduce-scatter.2.cloned.1.call-update
  308.6 139.4 %reduce-scatter.2.cloned.1.call-done = bf16[64,640]{1,0:T(8,128)(2,1)} async-done(((bf16[2048,640]{1,0:T(8,128)(2,1)}), bf16[64,640]{1,0:T(8,128)(2,1)}) %reduce-scatter.2.cloned.1.call-update) | async-done | bytes 81936 | tf_op jit(solution)/shard_map/reduce_scatter | solution.py:52
  447.9 10.0 %all_to_all.15 = bf16[8,8,640]{2,1,0:T(8,128)(2,1)S(1)} all-to-all(bf16[8,8,640]{2,1,0:T(8,128)(2,1)} %bitcast.51), channel_id=1, replica_groups=mesh['groups'=2,'ep'=32,'tp'=4,'dp'=2] {'tp','dp'}, dimensions={0} | all-to-all | bytes 163840 | tf_op jit(solution)/shard_map/all_to_all | solution.py:54
  458.0 0.6 copy.77
  (14 shorter events, 0.1 us)
Async XLA Ops:
  6.5 295.6 %copy-start = (bf16[1,1024,640]{2,1,0:T(8,128)(2,1)S(1)}, bf16[1,1024,640]{2,1,0:T(8,128)(2,1)}, u32[]{:S(2)}) copy-start(bf16[1,1024,640]{2,1,0:T(8,128)(2,1)} %param.11) | copy-start | bytes 3932164
  6.6 165.1 %all-gather.8.cloned.1.call-start = ((), (), s32[]{:S(2)}) async-start(), calls=%async_computation.4 | async-start | bytes 2770944 | tf_op jit(solution)/shard_map/all_gather | solution.py:27
  9.1 234.3 %all-gather.10.cloned.1.call-start = ((), (), s32[]{:S(2)}) async-start(), calls=%async_computation.5 | async-start | bytes 12091392 | tf_op jit(solution)/shard_map/all_gather | solution.py:39
  176.7 73.9 %copy-start.2 = (bf16[1,5120,128]{2,1,0:T(8,128)(2,1)S(1)}, bf16[1,5120,128]{2,1,0:T(8,128)(2,1)}, u32[]{:S(2)}) copy-start(bf16[1,5120,128]{2,1,0:T(8,128)(2,1)} %param.9) | copy-start | bytes 3932164
  176.7 125.4 %all-gather.6.cloned.1.call-start = ((), (), s32[]{:S(2)}) async-start(), calls=%async_computation.2 | async-start | bytes 2359296 | tf_op jit(solution)/shard_map/all_gather | solution.py:44
  250.6 4.1 copy-start.1
  250.6 4.1 copy-start.3
  258.4 189.5 %reduce-scatter.2.cloned.1.call-start = ((), (), s32[]{:S(2)}) async-start(), calls=%async_computation.3 | async-start | bytes 2703360 | tf_op jit(solution)/shard_map/reduce_scatter | solution.py:52
Sparse Core Ops, SparseCore 0:
  9.4 162.1 all-gather.7
  176.8 66.5 all-gather.9
  258.6 43.5 all-gather.5
  308.7 139.1 reduce-scatter.1
